TPU v7x, 32 devices: a whole 2x2x4 slice. The times are simulated.
32 devices in a mesh: row: 2 (over y), col: 16 (over z, x, core).
Axes of the slice: x: 2, y: 2, z: 4, core: 2. Of those that a mesh axis runs over, the one named last changes fastest.
Arguments:
- queries: bfloat16 [512, 4096], P(('row', 'col')), may hold values from -1.25 to 1.25
- passages: bfloat16 [8192, 4096], P(('col', 'row')), may hold values from -0.375 to 0.375
- positives: int32 [512], P('row'), may hold values from 0 to 8191, as said below
- hard_negatives: int32 [512, 7], P('row'), may hold values from 0 to 8191, as said below
- thresholds: float32 [512], P('row'), may hold values from 0.1 to 2
Outputs:
- row_losses: float32 [512], P(('row', 'col'))
- grad_queries: float32 [512, 4096], P(('row', 'col'))
- grad_passages: float32 [8192, 4096], P(('col', 'row'))
Inputs may be any that keep to these rules, and one draw needn't show every extreme that they name: `positives`: each query's positive passage. `hard_negatives`: passages mined for each query; ids may repeat or equal the query's positive.
All inputs are finite; a program needn't handle non-finite values.
Results may differ from a plain program's by a relative error of at most 0.0023.
Values may be sent and summed in bfloat16 or wider, within the bound.
A program may use at most 64 MiB of HBM per device.

v0:
```python
import functools
import jax
import jax.numpy as jnp
from jax import lax
from jax.experimental import pallas as pl
from jax.experimental.pallas import tpu as pltpu
from jax.sharding import PartitionSpec as P

inv_temp = 50.0
sharpness = 4.0


def combined_all(part, axis, combine):
    gathered = jax.tree.map(lambda a: lax.all_gather(a, axis), part)

    def take(source):
        return jax.tree.map(lambda a: lax.dynamic_index_in_dim(a, source, 0, False), gathered)

    return lax.fori_loop(
        1, lax.axis_size(axis), lambda source, state: combine(state, take(source)), take(0)
    )


def pair_merge(left_pair, right_pair):
    left_top, left_total = left_pair
    right_top, right_total = right_pair
    joined = jnp.maximum(left_top, right_top)
    return (
        joined,
        left_total * jnp.exp(left_top - joined) + right_total * jnp.exp(right_top - joined),
    )


def general_plan(queries, passages, positives, hard_negatives, thresholds):
    query_block = lax.all_gather(queries, "col", axis=0, tiled=True)
    passage_block = lax.all_gather(passages, "row", axis=0, tiled=True)
    block_width = passage_block.shape[0]
    query_rows = queries.shape[0]
    scores = jnp.dot(query_block, passage_block.T, preferred_element_type=jnp.float32) * inv_temp
    columns = lax.axis_index("col") * block_width + lax.iota(jnp.int32, block_width)
    positive_mask = positives[:, None] == columns[None, :]
    kept_mask = positive_mask
    for mined_slot in range(hard_negatives.shape[1]):
        kept_mask = kept_mask | (hard_negatives[:, mined_slot : mined_slot + 1] == columns[None, :])
    picked = lax.psum(jnp.sum(jnp.where(positive_mask, scores, 0.0), axis=1), "col")
    penalty = jax.nn.softplus(sharpness * (scores - picked[:, None] - thresholds[:, None]))
    logits = jnp.where(kept_mask, scores, scores - penalty)
    local_top = jnp.max(logits, axis=1)
    local_exp = jnp.exp(logits - local_top[:, None])
    row_top, denominator = combined_all((local_top, jnp.sum(local_exp, axis=1)), "col", pair_merge)
    shifted = local_exp * jnp.exp(local_top - row_top)[:, None]
    losses = row_top + jnp.log(denominator) - picked
    row_losses = lax.dynamic_slice_in_dim(losses, lax.axis_index("col") * query_rows, query_rows, 0)
    grad_scores = (
        (shifted / denominator[:, None] - positive_mask.astype(jnp.float32)) * inv_temp
    ).astype(jnp.bfloat16)
    query_full = jnp.dot(grad_scores, passage_block, preferred_element_type=jnp.float32)
    grad_queries = lax.psum_scatter(query_full, "col", scatter_dimension=0, tiled=True)
    passage_full = lax.dot_general(
        grad_scores, query_block, (((0,), (0,)), ((), ())), preferred_element_type=jnp.float32
    )
    grad_passages = lax.psum_scatter(passage_full, "row", scatter_dimension=0, tiled=True)
    return (row_losses, grad_queries, grad_passages)


cores = 2
lane = 128
fields = 16
MESH = pl.DeviceIdType.MESH


def step_kernel(
    rows, wide, deep, negs,
    q_ref, p_ref, positives_ref, mined_ref, thresholds_ref,
    loss_ref, gq_ref, gp_ref,
    q_all, p_mate, mined_wide, meta_ref, meta_all, scores, pick_out, pick_all, stat_out, stat_all,
    part, part_low, gp_out, gp_in,
    diag_in_y, diag_in_x, merge_x, merge_y, in_x, in_y, plane, z_out, z_in, z_out_full, z_in_full,
    own_send, fwd_send, diag_send, q_recv, qd_recv,
    mate_send, mate_recv, meta_send, meta_recv,
    pick_send, pick_recv, stat_send, stat_recv,
    rd_send, rd_recv, ru_send, ru_recv, rm_send, rm_recv, z_send, z_recv,
):
    y = lax.axis_index("row")
    col = lax.axis_index("col")
    core = lax.rem(col, cores)
    chip = col // cores
    z = chip // wide
    x = lax.rem(chip, wide)
    block, depth = q_ref.shape
    half = depth // 2
    own = p_ref.shape[0]
    groups = rows * deep * wide
    queries = groups * block

    def device(yy, zz, xx, cc=None):
        return (yy, (zz * wide + xx) * cores + (core if cc is None else cc))

    def slot(yy, zz, xx):
        return (yy * deep + zz) * wide + xx

    def span(g):
        return pl.ds(pl.multiple_of(g * block, block), block)

    def turn(at, by, size):
        return lax.rem(at + by, size)

    def send(src, dst, send_sem, recv_sem, to):
        copy = pltpu.make_async_remote_copy(
            src_ref=src, dst_ref=dst, send_sem=send_sem, recv_sem=recv_sem,
            device_id=to, device_id_type=MESH,
        )
        copy.start()
        sent.append(copy)

    def landed(ref, sem):
        pltpu.make_async_copy(ref, ref, sem).wait()

    sent = []
    left, right = pl.ds(0, half), pl.ds(half, half)
    yn, xn = turn(y, 1, rows), turn(x, 1, wide)
    me = slot(y, z, x)
    mate = device(y, z, x, 1 - core)
    peers = [
        (turn(y, a, rows), turn(z, b, deep), turn(x, d, wide))
        for b in range(deep) for a in range(rows) for d in range(wide) if a + b + d
    ]

    barrier = pltpu.get_barrier_semaphore()
    for peer in peers:
        pl.semaphore_signal(barrier, inc=1, device_id=device(*peer), device_id_type=MESH)
    pl.semaphore_signal(barrier, inc=1, device_id=mate, device_id_type=MESH)
    pl.semaphore_wait(barrier, len(peers) + 1)

    for b in range(1, deep):
        send(q_ref, q_all.at[span(me)], own_send.at[b], q_recv.at[me], device(y, turn(z, b, deep), x))
    send(q_ref, q_all.at[span(me)], own_send.at[0], q_recv.at[me], device(y, z, xn))
    send(q_ref, q_all.at[span(me)], own_send.at[deep], q_recv.at[me], device(yn, z, x))
    send(p_ref, p_mate, mate_send.at[0], mate_recv.at[0], mate)
    q_all[span(me), :] = q_ref[...]

    def mine(table):
        return jnp.concatenate(
            [table[(m * cores) * block : (m * cores + 1) * block] for m in range(deep * wide)], axis=0
        ), jnp.concatenate(
            [table[(m * cores + 1) * block : (m * cores + 2) * block] for m in range(deep * wide)], axis=0
        )

    mined_wide[...] = jnp.zeros_like(mined_wide)
    mined_wide[:negs, :] = mined_ref[...].astype(jnp.float32)
    mined_wide[fields // 2 : fields // 2 + 1, :] = positives_ref[...].astype(jnp.float32)
    mined_wide[fields // 2 + 1 : fields // 2 + 2, :] = thresholds_ref[...]
    one_first, one_second = mine(jnp.transpose(mined_wide[...]))
    meta_ref[...] = jnp.transpose(jnp.where(core == 0, one_first, one_second))[:fields]
    meta_all[y] = meta_ref[...]
    send(meta_ref, meta_all.at[y], meta_send, meta_recv, device(yn, z, x))
    def forward(b):
        g = slot(y, turn(z, b, deep), x)
        landed(q_all.at[span(g)], q_recv.at[g])
        send(q_all.at[span(g)], q_all.at[span(g)], fwd_send.at[b, 0], q_recv.at[g], device(y, z, xn))
        send(q_all.at[span(g)], q_all.at[span(g)], fwd_send.at[b, 1], q_recv.at[g], device(yn, z, x))

    def corner(b):
        zb = turn(z, b, deep)
        gx, gy = slot(y, zb, xn), slot(yn, zb, x)
        landed(q_all.at[span(gx)], q_recv.at[gx])
        send(
            q_all.at[span(gx), left], q_all.at[span(gx), left],
            diag_send.at[b, 0], qd_recv.at[zb, 0], device(yn, z, x),
        )
        landed(q_all.at[span(gy)], q_recv.at[gy])
        send(
            q_all.at[span(gy), right], q_all.at[span(gy), right],
            diag_send.at[b, 1], qd_recv.at[zb, 1], device(y, z, xn),
        )

    for b in range(1, deep):
        forward(b)
        corner(b - 1)
    corner(deep - 1)
    landed(p_mate, mate_recv.at[0])
    landed(meta_all.at[yn], meta_recv)
    for b in range(deep):
        zb = turn(z, b, deep)
        gd = slot(yn, zb, xn)
        landed(q_all.at[span(gd), left], qd_recv.at[zb, 0])
        landed(q_all.at[span(gd), right], qd_recv.at[zb, 1])

    scores[...] = jnp.zeros_like(scores)
    pieces = 4
    piece = depth // pieces

    @pl.loop(0, pieces)
    def _(k):
        ks = pl.ds(pl.multiple_of(k * piece, lane), piece)
        q_piece = q_all[:, ks]
        scores[:own, :] += lax.dot_general(
            p_ref[:, ks], q_piece, (((1,), (1,)), ((), ())), preferred_element_type=jnp.float32
        )
        scores[own:, :] += lax.dot_general(
            p_mate[:, ks], q_piece, (((1,), (1,)), ((), ())), preferred_element_type=jnp.float32
        )

    mt = jnp.concatenate([meta_all[a] for a in range(rows)], axis=1)
    at = lax.broadcasted_iota(jnp.int32, (2 * own, queries), 0)
    first = ((chip * cores + core) * rows + y) * own
    second = ((chip * cores + (1 - core)) * rows + y) * own
    ids = jnp.where(at < own, at + first, at - own + second).astype(jnp.float32)
    sc = scores[...] * inv_temp
    positive = ids == mt[fields // 2 : fields // 2 + 1, :]
    picked_here = jnp.sum(jnp.where(positive, sc, 0.0), axis=0, keepdims=True)
    pick_out[...] = picked_here
    for n, peer in enumerate(peers):
        send(pick_out, pick_all.at[me], pick_send.at[n], pick_recv.at[me], device(*peer))
    kept = positive
    for n in range(negs):
        kept = kept | (ids == mt[n : n + 1, :])
    pick_all[me] = picked_here
    for peer in peers:
        g = slot(*peer)
        landed(pick_all.at[g], pick_recv.at[g])
    picked = jnp.sum(pick_all[...], axis=0)
    v = sharpness * (sc - picked - mt[fields // 2 + 1 : fields // 2 + 2, :])
    penalty = jnp.maximum(v, 0.0) + jnp.log1p(jnp.exp(-jnp.abs(v)))
    logits = jnp.where(kept, sc, sc - penalty)
    top_here = jnp.max(logits, axis=0, keepdims=True)
    grown = jnp.exp(logits - top_here)
    sum_here = jnp.sum(grown, axis=0, keepdims=True)
    stat_out[...] = jnp.concatenate([top_here, sum_here], axis=1)
    for n, peer in enumerate(peers):
        send(stat_out, stat_all.at[me], stat_send.at[n], stat_recv.at[me], device(*peer))
    stat_all[me] = stat_out[...]
    for peer in peers:
        g = slot(*peer)
        landed(stat_all.at[g], stat_recv.at[g])
    stats = stat_all[...]
    tops, sums = stats[:, :, :queries], stats[:, :, queries:]
    row_top = jnp.max(tops, axis=0)
    total = jnp.sum(sums * jnp.exp(tops - row_top[None]), axis=0)
    losses = jnp.broadcast_to(row_top + jnp.log(total) - picked, (8, queries))
    loss_ref[...] = pltpu.roll(losses, lax.rem(queries - me * block, queries), 1)[:1, :lane]
    factor = jnp.exp(top_here - row_top) / total
    grad = ((grown * factor - positive.astype(jnp.float32)) * inv_temp).astype(jnp.bfloat16)
    grad_t = jnp.transpose(grad)

    cuts = 8
    cut = depth // cuts

    @pl.loop(0, cuts)
    def _(k):
        ks = pl.ds(pl.multiple_of(k * cut, lane), cut)
        value = jnp.dot(grad_t[:, :own], p_ref[:, ks], preferred_element_type=jnp.float32) + jnp.dot(
            grad_t[:, own:], p_mate[:, ks], preferred_element_type=jnp.float32
        )
        part[:, ks] = value
        part_low[:, ks] = value.astype(jnp.bfloat16)

    order = list(range(1, deep)) + [0]

    def diagonal(b):
        gd = slot(yn, turn(z, b, deep), xn)
        send(part_low.at[span(gd), left], diag_in_y.at[b], rd_send.at[b, 0], rd_recv.at[b, 0], device(yn, z, x))
        send(part_low.at[span(gd), right], diag_in_x.at[b], rd_send.at[b, 1], rd_recv.at[b, 1], device(y, z, xn))

    def plain(b):
        zb = turn(z, b, deep)
        gx, gy = slot(y, zb, xn), slot(yn, zb, x)
        send(part_low.at[span(gx), right], in_x.at[b, :, right], ru_send.at[b, 0], ru_recv.at[b, 0], device(y, z, xn))
        send(part_low.at[span(gy), left], in_y.at[b, :, left], ru_send.at[b, 1], ru_recv.at[b, 1], device(yn, z, x))

    def merged(b):
        zb = turn(z, b, deep)
        gx, gy = slot(y, zb, xn), slot(yn, zb, x)
        landed(diag_in_y.at[b], rd_recv.at[b, 0])
        merge_x[b] = (part[span(gx), left] + diag_in_y[b].astype(jnp.float32)).astype(jnp.bfloat16)
        send(merge_x.at[b], in_x.at[b, :, left], rm_send.at[b, 0], rm_recv.at[b, 0], device(y, z, xn))
        landed(diag_in_x.at[b], rd_recv.at[b, 1])
        merge_y[b] = (part[span(gy), right] + diag_in_x[b].astype(jnp.float32)).astype(jnp.bfloat16)
        send(merge_y.at[b], in_y.at[b, :, right], rm_send.at[b, 1], rm_recv.at[b, 1], device(yn, z, x))

    def z_buffers(b):
        return (z_out_full, z_in_full) if b in (1, deep - 1) else (z_out, z_in)

    def settle(b):
        zb = turn(z, b, deep)
        landed(in_x.at[b, :, right], ru_recv.at[b, 0])
        landed(in_y.at[b, :, left], ru_recv.at[b, 1])
        landed(in_x.at[b, :, left], rm_recv.at[b, 0])
        landed(in_y.at[b, :, right], rm_recv.at[b, 1])
        value = part[span(slot(y, zb, x)), :] + in_x[b].astype(jnp.float32) + in_y[b].astype(jnp.float32)
        if b:
            out, into = z_buffers(b)
            out[b] = value.astype(out.dtype)
            send(out.at[b], into.at[b], z_send.at[b], z_recv.at[b], device(y, zb, x))
        else:
            plane[...] = value

    diagonal(order[0])
    diagonal(order[1])
    plain(order[0])

    @pl.loop(0, cuts)
    def _(k):
        ks = pl.ds(pl.multiple_of(k * cut, lane), cut)
        gp_out[:, ks] = jnp.dot(grad[own:, :], q_all[:, ks], preferred_element_type=jnp.float32)

    send(gp_out, gp_in, mate_send.at[1], mate_recv.at[1], mate)

    for n, b in enumerate(order):
        merged(b)
        if n + 2 < deep:
            diagonal(order[n + 2])
        if n + 1 < deep:
            plain(order[n + 1])
        if n:
            settle(order[n - 1])

    @pl.loop(0, cuts)
    def _(k):
        ks = pl.ds(pl.multiple_of(k * cut, lane), cut)
        gp_ref[:, ks] = jnp.dot(grad[:own, :], q_all[:, ks], preferred_element_type=jnp.float32)

    landed(gp_in, mate_recv.at[1])

    @pl.loop(0, cuts)
    def _(k):
        ks = pl.ds(pl.multiple_of(k * cut, lane), cut)
        gp_ref[:, ks] += gp_in[:, ks]

    settle(0)
    value = plane[...]
    for b in range(1, deep):
        into = z_buffers(b)[1]
        landed(into.at[b], z_recv.at[b])
        value = value + into[b].astype(jnp.float32)
    gq_ref[...] = value
    for copy in sent:
        copy.wait_send()


def on_device(queries, passages, positives, hard_negatives, thresholds):
    rows, columns = lax.axis_size("row"), lax.axis_size("col")
    wide = rows
    deep = columns // (cores * wide)
    block, depth = queries.shape
    own = passages.shape[0]
    negs = hard_negatives.shape[1]
    run = deep * wide * block
    fits = rows == 2 and columns % (cores * wide) == 0 and deep > 1
    fits = fits and block % 16 == 0 and run % lane == 0 and negs <= fields // 2 and depth % 1024 == 0
    if not fits:
        return general_plan(queries, passages, positives, hard_negatives, thresholds)
    groups = rows * deep * wide
    total = groups * block
    half = depth // 2
    low, full = jnp.bfloat16, jnp.float32
    dma = pltpu.SemaphoreType.DMA
    losses, grad_queries, grad_passages = pl.pallas_call(
        functools.partial(step_kernel, rows, wide, deep, negs),
        out_shape=(
            jax.ShapeDtypeStruct((1, lane), full),
            jax.ShapeDtypeStruct((block, depth), full),
            jax.ShapeDtypeStruct((own, depth), full),
        ),
        in_specs=[pl.BlockSpec(memory_space=pltpu.VMEM)] * 5,
        out_specs=[pl.BlockSpec(memory_space=pltpu.VMEM)] * 3,
        scratch_shapes=[
            pltpu.VMEM((total, depth), low),
            pltpu.VMEM((own, depth), low),
            pltpu.VMEM((lane, columns * block), full),
            pltpu.VMEM((fields, run), full),
            pltpu.VMEM((rows, fields, run), full),
            pltpu.VMEM((cores * own, total), full),
            pltpu.VMEM((1, total), full),
            pltpu.VMEM((groups, 1, total), full),
            pltpu.VMEM((1, 2 * total), full),
            pltpu.VMEM((groups, 1, 2 * total), full),
            pltpu.VMEM((total, depth), full),
            pltpu.VMEM((total, depth), low),
            pltpu.VMEM((own, depth), full),
            pltpu.VMEM((own, depth), full),
            pltpu.VMEM((deep, block, half), low),
            pltpu.VMEM((deep, block, half), low),
            pltpu.VMEM((deep, block, half), low),
            pltpu.VMEM((deep, block, half), low),
            pltpu.VMEM((deep, block, depth), low),
            pltpu.VMEM((deep, block, depth), low),
            pltpu.VMEM((block, depth), full),
            pltpu.VMEM((deep, block, depth), low),
            pltpu.VMEM((deep, block, depth), low),
            pltpu.VMEM((deep, block, depth), full),
            pltpu.VMEM((deep, block, depth), full),
            dma((deep + 1,)), dma((deep, 2)), dma((deep, 2)), dma((groups,)), dma((deep, 2)),
            dma((2,)), dma((2,)), dma, dma,
            dma((groups,)), dma((groups,)), dma((groups,)), dma((groups,)),
            dma((deep, 2)), dma((deep, 2)), dma((deep, 2)), dma((deep, 2)),
            dma((deep, 2)), dma((deep, 2)), dma((deep,)), dma((deep,)),
        ],
        compiler_params=pltpu.CompilerParams(
            collective_id=0, has_side_effects=True, vmem_limit_bytes=38 * 1024 * 1024
        ),
    )(queries, passages, positives[None], hard_negatives.T, thresholds[None])
    return (losses[0, :block], grad_queries, grad_passages)


def solution(mesh):
    placed = (P(("row", "col"), None), P(("col", "row"), None), P("row"), P("row", None), P("row"))
    return jax.shard_map(
        on_device,
        mesh=mesh,
        in_specs=placed,
        out_specs=(P(("row", "col")), P(("row", "col"), None), P(("col", "row"), None)),
        check_vma=False,
    )
```

profile of v0, /device:TPU:0, one launch (start us, length us, event | category | flops | bytes accessed | tf_op | source)
XLA Modules:
  0.0 80.0 jit_solution(8814718502688745690)
XLA Ops:
  0.6 0.0 copy-start
  0.6 1.6 %copy-done = bf16[256,4096]{1,0:T(8,128)(2,1)S(1)} copy-done((bf16[256,4096]{1,0:T(8,128)(2,1)S(1)}, bf16[256,4096]{1,0:T(8,128)(2,1)}, u32[]{:S(2)}) %copy-start) | copy-done | bytes 2097176
  2.2 0.0 copy-start.1
  2.2 0.9 %copy-done.1 = bf16[16,4096]{1,0:T(8,128)(2,1)S(1)} copy-done((bf16[16,4096]{1,0:T(8,128)(2,1)S(1)}, bf16[16,4096]{1,0:T(8,128)(2,1)}, u32[]{:S(2)}) %copy-start.1) | copy-done | bytes 131096
  3.1 0.0 copy-start.2
  3.1 0.7 copy-done.2
  3.8 0.0 copy-start.3
  3.8 0.7 copy-done.3
  4.5 0.0 copy-start.4
  4.5 0.7 copy-done.4
  5.2 71.6 %shard_map.76 = (f32[1,128]{1,0:T(1,128)S(1)}, f32[16,4096]{1,0:T(8,128)S(1)}, f32[256,4096]{1,0:T(8,128)S(1)}) custom-call(bf16[16,4096]{1,0:T(8,128)(2,1)S(1)} %copy-done.1, bf16[256,4096]{1,0:T(8,128)(2,1)S(1)} %copy-done, s32[1,256]{1,0:T(1,128)S(1)} %bitcast.6, s32[7,256]{1,0:T(8,128)S(1)} %bitcast.5, f32[1,256]{1,0:T(1,128)S(1)} %bitcast.7), custom_call_target="tpu_custom_call" | custom-call | tf_op jit(solution)/shard_map/pallas_call | solution.py:358
  76.8 0.5 slice_bitcast_fusion
  77.3 0.7 copy.10
  78.0 2.0 %copy.11 = f32[256,4096]{1,0:T(8,128)} copy(f32[256,4096]{1,0:T(8,128)S(1)} %get-tuple-element.14) | data formatting | bytes 8388608
Async XLA Ops:
  0.6 1.6 %copy-start = (bf16[256,4096]{1,0:T(8,128)(2,1)S(1)}, bf16[256,4096]{1,0:T(8,128)(2,1)}, u32[]{:S(2)}) copy-start(bf16[256,4096]{1,0:T(8,128)(2,1)} %p_ref.1) | copy-start | bytes 6291460
  2.2 0.9 %copy-start.1 = (bf16[16,4096]{1,0:T(8,128)(2,1)S(1)}, bf16[16,4096]{1,0:T(8,128)(2,1)}, u32[]{:S(2)}) copy-start(bf16[16,4096]{1,0:T(8,128)(2,1)} %q_ref.1) | copy-start | bytes 393220
  3.1 0.7 copy-start.2
  3.8 0.7 copy-start.3
  4.5 0.7 copy-start.4
where the time goes:
time: 80.3 us; the launch traced here: 80 us
  Pallas kernels  71.6 us (89%)
  local copies, waits for them, and re-layouts  7.77 us (10%)
    pallas_call x1, Pallas kernels, on_device(): pl.pallas_call(functools.partial(step_kernel, rows, wide, deep, negs), ou...  71.6 us
    unnamed x12, local copies, waits for them, and re-layouts  7.26 us

commit v1 on v0

--- a/solution.py
+++ b/solution.py
@@ -73,10 +73,11 @@
     rows, wide, deep, negs,
     q_ref, p_ref, positives_ref, mined_ref, thresholds_ref,
     loss_ref, gq_ref, gp_ref,
+    p_own, positives_own, mined_own, thresholds_own,
     q_all, p_mate, mined_wide, meta_ref, meta_all, scores, pick_out, pick_all, stat_out, stat_all,
     part, part_low, gp_out, gp_in,
     diag_in_y, diag_in_x, merge_x, merge_y, in_x, in_y, plane, z_out, z_in, z_out_full, z_in_full,
-    own_send, fwd_send, diag_send, q_recv, qd_recv,
+    load_sem, own_send, fwd_send, diag_send, q_recv,
     mate_send, mate_recv, meta_send, meta_recv,
     pick_send, pick_recv, stat_send, stat_recv,
     rd_send, rd_recv, ru_send, ru_recv, rm_send, rm_recv, z_send, z_recv,
@@ -117,27 +118,79 @@
         pltpu.make_async_copy(ref, ref, sem).wait()
 
     sent = []
+    waits = []
     left, right = pl.ds(0, half), pl.ds(half, half)
     yn, xn = turn(y, 1, rows), turn(x, 1, wide)
     me = slot(y, z, x)
     mate = device(y, z, x, 1 - core)
+    across, along = device(y, z, xn), device(yn, z, x)
     peers = [
         (turn(y, a, rows), turn(z, b, deep), turn(x, d, wide))
         for b in range(deep) for a in range(rows) for d in range(wide) if a + b + d
     ]
-
+    steps = 4
+    width = depth // steps
+
+    def columns(k):
+        return pl.ds(k * width, width)
+
+    q_load = pltpu.make_async_copy(q_ref, q_all.at[span(me)], load_sem.at[0])
+    p_load = pltpu.make_async_copy(p_ref, p_own, load_sem.at[1])
+    tables = [
+        pltpu.make_async_copy(positives_ref, positives_own, load_sem.at[2]),
+        pltpu.make_async_copy(mined_ref, mined_own, load_sem.at[3]),
+        pltpu.make_async_copy(thresholds_ref, thresholds_own, load_sem.at[4]),
+    ]
+    q_load.start()
+    p_load.start()
+    for table in tables:
+        table.start()
+
+    has_up, has_down = z < deep - 1, z > 0
+    above = device(y, jnp.minimum(z + 1, deep - 1), x)
+    below = device(y, jnp.maximum(z - 1, 0), x)
     barrier = pltpu.get_barrier_semaphore()
-    for peer in peers:
-        pl.semaphore_signal(barrier, inc=1, device_id=device(*peer), device_id_type=MESH)
-    pl.semaphore_signal(barrier, inc=1, device_id=mate, device_id_type=MESH)
-    pl.semaphore_wait(barrier, len(peers) + 1)
-
-    for b in range(1, deep):
-        send(q_ref, q_all.at[span(me)], own_send.at[b], q_recv.at[me], device(y, turn(z, b, deep), x))
-    send(q_ref, q_all.at[span(me)], own_send.at[0], q_recv.at[me], device(y, z, xn))
-    send(q_ref, q_all.at[span(me)], own_send.at[deep], q_recv.at[me], device(yn, z, x))
-    send(p_ref, p_mate, mate_send.at[0], mate_recv.at[0], mate)
-    q_all[span(me), :] = q_ref[...]
+    for to in (across, along, mate):
+        pl.semaphore_signal(barrier, inc=1, device_id=to, device_id_type=MESH)
+
+    @pl.when(has_up)
+    def _():
+        pl.semaphore_signal(barrier, inc=1, device_id=above, device_id_type=MESH)
+
+    @pl.when(has_down)
+    def _():
+        pl.semaphore_signal(barrier, inc=1, device_id=below, device_id_type=MESH)
+
+    pl.semaphore_wait(barrier, 3 + jnp.where(has_up, 1, 0) + jnp.where(has_down, 1, 0))
+    q_load.wait()
+
+    def pass_on(g, k, sem, to):
+        ref = q_all.at[span(g), columns(k)]
+        pltpu.make_async_remote_copy(
+            src_ref=ref, dst_ref=ref, send_sem=sem, recv_sem=q_recv.at[g, k],
+            device_id=to, device_id_type=MESH,
+        ).start()
+
+    whole = q_all.at[span(me)]
+    for k in range(steps):
+        @pl.when(has_up)
+        def _():
+            pass_on(me, k, own_send.at[0], above)
+
+        @pl.when(has_down)
+        def _():
+            pass_on(me, k, own_send.at[1], below)
+
+        pass_on(me, k, own_send.at[2], across)
+        pass_on(me, k, own_send.at[3], along)
+    waits.append((has_up, whole, own_send.at[0]))
+    waits.append((has_down, whole, own_send.at[1]))
+    waits.append((None, whole, own_send.at[2]))
+    waits.append((None, whole, own_send.at[3]))
+    p_load.wait()
+    send(p_own, p_mate, mate_send.at[0], mate_recv.at[0], mate)
+    for table in tables:
+        table.wait()
 
     def mine(table):
         return jnp.concatenate(
@@ -147,59 +200,94 @@
         )
 
     mined_wide[...] = jnp.zeros_like(mined_wide)
-    mined_wide[:negs, :] = mined_ref[...].astype(jnp.float32)
-    mined_wide[fields // 2 : fields // 2 + 1, :] = positives_ref[...].astype(jnp.float32)
-    mined_wide[fields // 2 + 1 : fields // 2 + 2, :] = thresholds_ref[...]
+    mined_wide[:negs, :] = mined_own[...].astype(jnp.float32)
+    mined_wide[fields // 2 : fields // 2 + 1, :] = positives_own[...].astype(jnp.float32)
+    mined_wide[fields // 2 + 1 : fields // 2 + 2, :] = thresholds_own[...]
     one_first, one_second = mine(jnp.transpose(mined_wide[...]))
     meta_ref[...] = jnp.transpose(jnp.where(core == 0, one_first, one_second))[:fields]
     meta_all[y] = meta_ref[...]
     send(meta_ref, meta_all.at[y], meta_send, meta_recv, device(yn, z, x))
-    def forward(b):
-        g = slot(y, turn(z, b, deep), x)
-        landed(q_all.at[span(g)], q_recv.at[g])
-        send(q_all.at[span(g)], q_all.at[span(g)], fwd_send.at[b, 0], q_recv.at[g], device(y, z, xn))
-        send(q_all.at[span(g)], q_all.at[span(g)], fwd_send.at[b, 1], q_recv.at[g], device(yn, z, x))
-
-    def corner(b):
-        zb = turn(z, b, deep)
-        gx, gy = slot(y, zb, xn), slot(yn, zb, x)
-        landed(q_all.at[span(gx)], q_recv.at[gx])
-        send(
-            q_all.at[span(gx), left], q_all.at[span(gx), left],
-            diag_send.at[b, 0], qd_recv.at[zb, 0], device(yn, z, x),
-        )
-        landed(q_all.at[span(gy)], q_recv.at[gy])
-        send(
-            q_all.at[span(gy), right], q_all.at[span(gy), right],
-            diag_send.at[b, 1], qd_recv.at[zb, 1], device(y, z, xn),
-        )
-
-    for b in range(1, deep):
-        forward(b)
-        corner(b - 1)
-    corner(deep - 1)
+
+    def column_step(h, up):
+        source = z - h if up else z + h
+        inside = source >= 0 if up else source < deep
+        more = has_up if up else has_down
+        far = above if up else below
+        g = slot(y, jnp.clip(source, 0, deep - 1), x)
+        sems = fwd_send.at[0 if up else 1, h - 1]
+
+        def arrive(k):
+            @pl.when(inside)
+            def _():
+                landed(q_all.at[span(g), columns(k)], q_recv.at[g, k])
+
+                @pl.when(more)
+                def _():
+                    pass_on(g, k, sems.at[0], far)
+
+                pass_on(g, k, sems.at[1], across)
+                pass_on(g, k, sems.at[2], along)
+
+        waits.append((inside & more, whole, sems.at[0]))
+        waits.append((inside, whole, sems.at[1]))
+        waits.append((inside, whole, sems.at[2]))
+        return arrive
+
+    def corner_step(source, inside, sem):
+        at = jnp.clip(source, 0, deep - 1)
+        gx, gy = slot(y, at, xn), slot(yn, at, x)
+
+        def forward(k):
+            g, to, n = (gx, along, 0) if k % 2 == 0 else (gy, across, 1)
+
+            def go():
+                landed(q_all.at[span(g), columns(k)], q_recv.at[g, k])
+                pass_on(g, k, sem.at[n], to)
+
+            if inside is None:
+                go()
+            else:
+                pl.when(inside)(go)
+
+        waits.append((inside, q_all.at[span(me), left], sem.at[0]))
+        waits.append((inside, q_all.at[span(me), left], sem.at[1]))
+        return forward
+
+    corners = [corner_step(z, None, diag_send.at[0, 0])]
+    for h in range(1, deep):
+        arrivals = [column_step(h, True), column_step(h, False)]
+        for k in range(steps):
+            for go in arrivals:
+                go(k)
+            for go in corners:
+                go(k)
+        corners = [
+            corner_step(z - h, z - h >= 0, diag_send.at[0, h]),
+            corner_step(z + h, z + h < deep, diag_send.at[1, h]),
+        ]
+    for k in range(steps):
+        for go in corners:
+            go(k)
     landed(p_mate, mate_recv.at[0])
     landed(meta_all.at[yn], meta_recv)
-    for b in range(deep):
-        zb = turn(z, b, deep)
-        gd = slot(yn, zb, xn)
-        landed(q_all.at[span(gd), left], qd_recv.at[zb, 0])
-        landed(q_all.at[span(gd), right], qd_recv.at[zb, 1])
-
-    scores[...] = jnp.zeros_like(scores)
-    pieces = 4
-    piece = depth // pieces
-
-    @pl.loop(0, pieces)
-    def _(k):
-        ks = pl.ds(pl.multiple_of(k * piece, lane), piece)
+
+    for k in range(steps):
+        for b in range(deep):
+            zb = turn(z, b, deep)
+            g = slot(yn, zb, x) if k % 2 == 0 else slot(y, zb, xn)
+            gd = slot(yn, zb, xn)
+            landed(q_all.at[span(g), columns(k)], q_recv.at[g, k])
+            landed(q_all.at[span(gd), columns(k)], q_recv.at[gd, k])
+        ks = columns(k)
         q_piece = q_all[:, ks]
-        scores[:own, :] += lax.dot_general(
-            p_ref[:, ks], q_piece, (((1,), (1,)), ((), ())), preferred_element_type=jnp.float32
-        )
-        scores[own:, :] += lax.dot_general(
-            p_mate[:, ks], q_piece, (((1,), (1,)), ((), ())), preferred_element_type=jnp.float32
-        )
+        for at, p_part in ((0, p_own), (own, p_mate)):
+            value = lax.dot_general(
+                p_part[:, ks], q_piece, (((1,), (1,)), ((), ())), preferred_element_type=jnp.float32
+            )
+            if k:
+                scores[at : at + own, :] += value
+            else:
+                scores[at : at + own, :] = value
 
     mt = jnp.concatenate([meta_all[a] for a in range(rows)], axis=1)
     at = lax.broadcasted_iota(jnp.int32, (2 * own, queries), 0)
@@ -249,7 +337,7 @@
     @pl.loop(0, cuts)
     def _(k):
         ks = pl.ds(pl.multiple_of(k * cut, lane), cut)
-        value = jnp.dot(grad_t[:, :own], p_ref[:, ks], preferred_element_type=jnp.float32) + jnp.dot(
+        value = jnp.dot(grad_t[:, :own], p_own[:, ks], preferred_element_type=jnp.float32) + jnp.dot(
             grad_t[:, own:], p_mate[:, ks], preferred_element_type=jnp.float32
         )
         part[:, ks] = value
@@ -334,6 +422,11 @@
         landed(into.at[b], z_recv.at[b])
         value = value + into[b].astype(jnp.float32)
     gq_ref[...] = value
+    for inside, ref, sem in waits:
+        if inside is None:
+            landed(ref, sem)
+        else:
+            pl.when(inside)(functools.partial(landed, ref, sem))
     for copy in sent:
         copy.wait_send()
 
@@ -362,9 +455,13 @@
             jax.ShapeDtypeStruct((block, depth), full),
             jax.ShapeDtypeStruct((own, depth), full),
         ),
-        in_specs=[pl.BlockSpec(memory_space=pltpu.VMEM)] * 5,
+        in_specs=[pl.BlockSpec(memory_space=pltpu.HBM)] * 5,
         out_specs=[pl.BlockSpec(memory_space=pltpu.VMEM)] * 3,
         scratch_shapes=[
+            pltpu.VMEM((own, depth), low),
+            pltpu.VMEM((1, positives.shape[0]), jnp.int32),
+            pltpu.VMEM((negs, positives.shape[0]), jnp.int32),
+            pltpu.VMEM((1, positives.shape[0]), full),
             pltpu.VMEM((total, depth), low),
             pltpu.VMEM((own, depth), low),
             pltpu.VMEM((lane, columns * block), full),
@@ -390,14 +487,14 @@
             pltpu.VMEM((deep, block, depth), low),
             pltpu.VMEM((deep, block, depth), full),
             pltpu.VMEM((deep, block, depth), full),
-            dma((deep + 1,)), dma((deep, 2)), dma((deep, 2)), dma((groups,)), dma((deep, 2)),
+            dma((5,)), dma((4,)), dma((2, deep, 3)), dma((2, deep, 2)), dma((groups, 4)),
             dma((2,)), dma((2,)), dma, dma,
             dma((groups,)), dma((groups,)), dma((groups,)), dma((groups,)),
             dma((deep, 2)), dma((deep, 2)), dma((deep, 2)), dma((deep, 2)),
             dma((deep, 2)), dma((deep, 2)), dma((deep,)), dma((deep,)),
         ],
         compiler_params=pltpu.CompilerParams(
-            collective_id=0, has_side_effects=True, vmem_limit_bytes=38 * 1024 * 1024
+            collective_id=0, has_side_effects=True, vmem_limit_bytes=44 * 1024 * 1024
         ),
     )(queries, passages, positives[None], hard_negatives.T, thresholds[None])
     return (losses[0, :block], grad_queries, grad_passages)

time: 80.3 us -> 69.9 us (0.87)
  Pallas kernels: 71.6 us -> 61.3 us
    pallas_call x1, Pallas kernels: 71.6 us -> 61.3 us  [on_device(): pl.pallas_call(functools.partial(step_kernel, rows, wide, deep, negs), ou...]
where the time goes in v1:
time: 69.9 us; the launch traced here: 69.7 us
  Pallas kernels  61.3 us (88%)
  local copies, waits for them, and re-layouts  7.77 us (11%)
    pallas_call x1, Pallas kernels, on_device(): pl.pallas_call(functools.partial(step_kernel, rows, wide, deep, negs), ou...  61.3 us
    unnamed x12, local copies, waits for them, and re-layouts  7.26 us

profile of v1, /device:TPU:0, one launch (start us, length us, event | category | flops | bytes accessed | tf_op | source)
XLA Modules:
  0.0 69.7 jit_solution(333812821948252286)
XLA Ops:
  0.6 0.0 copy-start
  0.6 1.6 %copy-done = bf16[256,4096]{1,0:T(8,128)(2,1)S(1)} copy-done((bf16[256,4096]{1,0:T(8,128)(2,1)S(1)}, bf16[256,4096]{1,0:T(8,128)(2,1)}, u32[]{:S(2)}) %copy-start) | copy-done | bytes 2097176
  2.2 0.0 copy-start.1
  2.2 0.9 %copy-done.1 = bf16[16,4096]{1,0:T(8,128)(2,1)S(1)} copy-done((bf16[16,4096]{1,0:T(8,128)(2,1)S(1)}, bf16[16,4096]{1,0:T(8,128)(2,1)}, u32[]{:S(2)}) %copy-start.1) | copy-done | bytes 131096
  3.1 0.0 copy-start.2
  3.1 0.7 copy-done.2
  3.8 0.0 copy-start.3
  3.8 0.7 copy-done.3
  4.5 0.0 copy-start.4
  4.5 0.7 copy-done.4
  5.2 61.3 %shard_map.76 = (f32[1,128]{1,0:T(1,128)S(1)}, f32[16,4096]{1,0:T(8,128)S(1)}, f32[256,4096]{1,0:T(8,128)S(1)}) custom-call(bf16[16,4096]{1,0:T(8,128)(2,1)S(1)} %copy-done.1, bf16[256,4096]{1,0:T(8,128)(2,1)S(1)} %copy-done, s32[1,256]{1,0:T(1,128)S(1)} %bitcast.6, s32[7,256]{1,0:T(8,128)S(1)} %bitcast.5, f32[1,256]{1,0:T(1,128)S(1)} %bitcast.7), custom_call_target="tpu_custom_call" | custom-call | tf_op jit(solution)/shard_map/pallas_call | solution.py:451
  66.5 0.5 slice_bitcast_fusion
  67.0 0.7 %copy.10 = f32[16,4096]{1,0:T(8,128)} copy(f32[16,4096]{1,0:T(8,128)S(1)} %get-tuple-element.13) | data formatting | bytes 524288
  67.7 2.0 %copy.11 = f32[256,4096]{1,0:T(8,128)} copy(f32[256,4096]{1,0:T(8,128)S(1)} %get-tuple-element.14) | data formatting | bytes 8388608
Async XLA Ops:
  0.6 1.6 %copy-start = (bf16[256,4096]{1,0:T(8,128)(2,1)S(1)}, bf16[256,4096]{1,0:T(8,128)(2,1)}, u32[]{:S(2)}) copy-start(bf16[256,4096]{1,0:T(8,128)(2,1)} %p_ref.1) | copy-start | bytes 6291460
  2.2 0.9 %copy-start.1 = (bf16[16,4096]{1,0:T(8,128)(2,1)S(1)}, bf16[16,4096]{1,0:T(8,128)(2,1)}, u32[]{:S(2)}) copy-start(bf16[16,4096]{1,0:T(8,128)(2,1)} %q_ref.1) | copy-start | bytes 393220
  3.1 0.7 copy-start.2
  3.8 0.7 copy-start.3
  4.5 0.7 copy-start.4

commit v2 on v1

--- a/solution.py
+++ b/solution.py
@@ -80,7 +80,7 @@
     load_sem, own_send, fwd_send, diag_send, q_recv,
     mate_send, mate_recv, meta_send, meta_recv,
     pick_send, pick_recv, stat_send, stat_recv,
-    rd_send, rd_recv, ru_send, ru_recv, rm_send, rm_recv, z_send, z_recv,
+    rd_send, rd_recv, ru_send, ru_recv, rm_send, rm_recv, z_send, z_recv, turn_sem,
 ):
     y = lax.axis_index("row")
     col = lax.axis_index("col")
@@ -172,6 +172,11 @@
         ).start()
 
     whole = q_all.at[span(me)]
+
+    @pl.when(core == 0)
+    def _():
+        pl.semaphore_wait(turn_sem, 1)
+
     for k in range(steps):
         @pl.when(has_up)
         def _():
@@ -261,6 +266,11 @@
                 go(k)
             for go in corners:
                 go(k)
+        if h == 1:
+            @pl.when(core == 1)
+            def _():
+                pl.semaphore_signal(turn_sem, inc=1, device_id=mate, device_id_type=MESH)
+
         corners = [
             corner_step(z - h, z - h >= 0, diag_send.at[0, h]),
             corner_step(z + h, z + h < deep, diag_send.at[1, h]),
@@ -297,95 +307,128 @@
     sc = scores[...] * inv_temp
     positive = ids == mt[fields // 2 : fields // 2 + 1, :]
     picked_here = jnp.sum(jnp.where(positive, sc, 0.0), axis=0, keepdims=True)
-    pick_out[...] = picked_here
-    for n, peer in enumerate(peers):
-        send(pick_out, pick_all.at[me], pick_send.at[n], pick_recv.at[me], device(*peer))
     kept = positive
     for n in range(negs):
         kept = kept | (ids == mt[n : n + 1, :])
-    pick_all[me] = picked_here
+    held_here = jnp.max(jnp.where(kept, sc, -jnp.inf), axis=0, keepdims=True)
+    pick_out[...] = jnp.concatenate([picked_here, held_here], axis=1)
+    for n, peer in enumerate(peers):
+        send(pick_out, pick_all.at[me], pick_send.at[n], pick_recv.at[me], device(*peer))
+    pick_all[me] = pick_out[...]
     for peer in peers:
         g = slot(*peer)
         landed(pick_all.at[g], pick_recv.at[g])
-    picked = jnp.sum(pick_all[...], axis=0)
+    picks = pick_all[...]
+    picked = jnp.sum(picks[:, :, :queries], axis=0)
+    held = jnp.max(picks[:, :, queries:], axis=0)
     v = sharpness * (sc - picked - mt[fields // 2 + 1 : fields // 2 + 2, :])
     penalty = jnp.maximum(v, 0.0) + jnp.log1p(jnp.exp(-jnp.abs(v)))
-    logits = jnp.where(kept, sc, sc - penalty)
-    top_here = jnp.max(logits, axis=0, keepdims=True)
-    grown = jnp.exp(logits - top_here)
+    grown = jnp.exp(jnp.where(kept, sc, sc - penalty) - held)
     sum_here = jnp.sum(grown, axis=0, keepdims=True)
-    stat_out[...] = jnp.concatenate([top_here, sum_here], axis=1)
+    stat_out[...] = sum_here
     for n, peer in enumerate(peers):
         send(stat_out, stat_all.at[me], stat_send.at[n], stat_recv.at[me], device(*peer))
-    stat_all[me] = stat_out[...]
+    stat_all[me] = sum_here
     for peer in peers:
         g = slot(*peer)
         landed(stat_all.at[g], stat_recv.at[g])
-    stats = stat_all[...]
-    tops, sums = stats[:, :, :queries], stats[:, :, queries:]
-    row_top = jnp.max(tops, axis=0)
-    total = jnp.sum(sums * jnp.exp(tops - row_top[None]), axis=0)
-    losses = jnp.broadcast_to(row_top + jnp.log(total) - picked, (8, queries))
-    loss_ref[...] = pltpu.roll(losses, lax.rem(queries - me * block, queries), 1)[:1, :lane]
-    factor = jnp.exp(top_here - row_top) / total
+    total = jnp.sum(stat_all[...], axis=0)
+    losses = jnp.broadcast_to(held + jnp.log(total) - picked, (8, queries))
+    loss_ref[...] = pltpu.roll(losses, lax.rem(queries - me * block, queries), 1)[:1, :block]
+    factor = 1.0 / total
     grad = ((grown * factor - positive.astype(jnp.float32)) * inv_temp).astype(jnp.bfloat16)
     grad_t = jnp.transpose(grad)
 
     cuts = 8
     cut = depth // cuts
-
-    @pl.loop(0, cuts)
-    def _(k):
-        ks = pl.ds(pl.multiple_of(k * cut, lane), cut)
-        value = jnp.dot(grad_t[:, :own], p_own[:, ks], preferred_element_type=jnp.float32) + jnp.dot(
-            grad_t[:, own:], p_mate[:, ks], preferred_element_type=jnp.float32
-        )
-        part[:, ks] = value
-        part_low[:, ks] = value.astype(jnp.bfloat16)
-
-    order = list(range(1, deep)) + [0]
-
-    def diagonal(b):
-        gd = slot(yn, turn(z, b, deep), xn)
-        send(part_low.at[span(gd), left], diag_in_y.at[b], rd_send.at[b, 0], rd_recv.at[b, 0], device(yn, z, x))
-        send(part_low.at[span(gd), right], diag_in_x.at[b], rd_send.at[b, 1], rd_recv.at[b, 1], device(y, z, xn))
-
-    def plain(b):
-        zb = turn(z, b, deep)
-        gx, gy = slot(y, zb, xn), slot(yn, zb, x)
-        send(part_low.at[span(gx), right], in_x.at[b, :, right], ru_send.at[b, 0], ru_recv.at[b, 0], device(y, z, xn))
-        send(part_low.at[span(gy), left], in_y.at[b, :, left], ru_send.at[b, 1], ru_recv.at[b, 1], device(yn, z, x))
-
-    def merged(b):
-        zb = turn(z, b, deep)
-        gx, gy = slot(y, zb, xn), slot(yn, zb, x)
-        landed(diag_in_y.at[b], rd_recv.at[b, 0])
-        merge_x[b] = (part[span(gx), left] + diag_in_y[b].astype(jnp.float32)).astype(jnp.bfloat16)
-        send(merge_x.at[b], in_x.at[b, :, left], rm_send.at[b, 0], rm_recv.at[b, 0], device(y, z, xn))
-        landed(diag_in_x.at[b], rd_recv.at[b, 1])
-        merge_y[b] = (part[span(gy), right] + diag_in_x[b].astype(jnp.float32)).astype(jnp.bfloat16)
-        send(merge_y.at[b], in_y.at[b, :, right], rm_send.at[b, 1], rm_recv.at[b, 1], device(yn, z, x))
-
-    def z_buffers(b):
-        return (z_out_full, z_in_full) if b in (1, deep - 1) else (z_out, z_in)
-
-    def settle(b):
-        zb = turn(z, b, deep)
-        landed(in_x.at[b, :, right], ru_recv.at[b, 0])
-        landed(in_y.at[b, :, left], ru_recv.at[b, 1])
-        landed(in_x.at[b, :, left], rm_recv.at[b, 0])
-        landed(in_y.at[b, :, right], rm_recv.at[b, 1])
-        value = part[span(slot(y, zb, x)), :] + in_x[b].astype(jnp.float32) + in_y[b].astype(jnp.float32)
-        if b:
-            out, into = z_buffers(b)
-            out[b] = value.astype(out.dtype)
-            send(out.at[b], into.at[b], z_send.at[b], z_recv.at[b], device(y, zb, x))
+    parts = 4
+    share = depth // parts
+    per = parts // 2
+    mix = [k for pair in zip(range(per), range(per, parts)) for k in pair]
+    low_half = z < deep // 2
+    folded = jnp.where(low_half, z, deep - 1 - z)
+
+    def target(n):
+        if n == deep - 1:
+            return z
+        v = deep - 1 - n
+        v = jnp.where(v > folded, v, v - 1)
+        return jnp.where(low_half, v, deep - 1 - v)
+
+    targets = [target(n) for n in range(deep)]
+
+    def area(k, wrap=False):
+        return pl.ds((k % per if wrap else k) * share, share)
+
+    def post(src, dst, send_sem, recv_sem, to):
+        pltpu.make_async_remote_copy(
+            src_ref=src, dst_ref=dst, send_sem=send_sem, recv_sem=recv_sem,
+            device_id=to, device_id_type=MESH,
+        ).start()
+
+    def route(k):
+        return (along, across) if k < per else (across, along)
+
+    def diagonal(n, k):
+        gd = slot(yn, targets[n], xn)
+        into = diag_in_y if k < per else diag_in_x
+        post(
+            part_low.at[span(gd), area(k)], into.at[n, :, area(k, True)],
+            rd_send.at[n, k // per], rd_recv.at[n, k], route(k)[0],
+        )
+
+    def plain(n, k):
+        g, into = (slot(yn, targets[n], x), in_y) if k < per else (slot(y, targets[n], xn), in_x)
+        post(
+            part_low.at[span(g), area(k)], into.at[n, :, area(k)],
+            ru_send.at[n, k // per], ru_recv.at[n, k], route(k)[0],
+        )
+
+    def merged(n, k):
+        g = slot(y, targets[n], xn) if k < per else slot(yn, targets[n], x)
+        got, out, into = (diag_in_y, merge_x, in_x) if k < per else (diag_in_x, merge_y, in_y)
+        landed(got.at[n, :, area(k, True)], rd_recv.at[n, k])
+        out[n, :, area(k, True)] = (
+            part[span(g), area(k)] + got[n, :, area(k, True)].astype(jnp.float32)
+        ).astype(jnp.bfloat16)
+        post(
+            out.at[n, :, area(k, True)], into.at[n, :, area(k)],
+            rm_send.at[n, k // per], rm_recv.at[n, k], route(k)[1],
+        )
+
+    def z_buffers(n):
+        return (z_out_full, z_in_full) if n >= deep // 2 else (z_out, z_in)
+
+    def settle(n, k):
+        landed((in_y if k < per else in_x).at[n, :, area(k)], ru_recv.at[n, k])
+        landed((in_x if k < per else in_y).at[n, :, area(k)], rm_recv.at[n, k])
+        g = slot(y, targets[n], x)
+        value = (
+            part[span(g), area(k)]
+            + in_x[n, :, area(k)].astype(jnp.float32)
+            + in_y[n, :, area(k)].astype(jnp.float32)
+        )
+        if n < deep - 1:
+            out, into = z_buffers(n)
+            out[n, :, area(k)] = value.astype(out.dtype)
+            post(
+                out.at[n, :, area(k)], into.at[z, :, area(k)],
+                z_send.at[n], z_recv.at[z, k], device(y, targets[n], x),
+            )
         else:
-            plane[...] = value
-
-    diagonal(order[0])
-    diagonal(order[1])
-    plain(order[0])
+            plane[:, area(k)] = value
+
+    for k in mix:
+        value = jnp.dot(grad_t[:, :own], p_own[:, area(k)], preferred_element_type=jnp.float32) + jnp.dot(
+            grad_t[:, own:], p_mate[:, area(k)], preferred_element_type=jnp.float32
+        )
+        part[:, area(k)] = value
+        part_low[:, area(k)] = value.astype(jnp.bfloat16)
+        diagonal(0, k)
+    for k in mix:
+        diagonal(1, k)
+    for k in mix:
+        plain(0, k)
 
     @pl.loop(0, cuts)
     def _(k):
@@ -394,34 +437,41 @@
 
     send(gp_out, gp_in, mate_send.at[1], mate_recv.at[1], mate)
 
-    for n, b in enumerate(order):
-        merged(b)
-        if n + 2 < deep:
-            diagonal(order[n + 2])
+    for n in range(deep):
+        for k in mix:
+            merged(n, k)
+            if n + 2 < deep:
+                diagonal(n + 2, k)
         if n + 1 < deep:
-            plain(order[n + 1])
+            for k in mix:
+                plain(n + 1, k)
         if n:
-            settle(order[n - 1])
+            for k in mix:
+                settle(n - 1, k)
+
+    landed(gp_in, mate_recv.at[1])
 
     @pl.loop(0, cuts)
     def _(k):
         ks = pl.ds(pl.multiple_of(k * cut, lane), cut)
-        gp_ref[:, ks] = jnp.dot(grad[:own, :], q_all[:, ks], preferred_element_type=jnp.float32)
-
-    landed(gp_in, mate_recv.at[1])
-
-    @pl.loop(0, cuts)
-    def _(k):
-        ks = pl.ds(pl.multiple_of(k * cut, lane), cut)
-        gp_ref[:, ks] += gp_in[:, ks]
-
-    settle(0)
-    value = plane[...]
-    for b in range(1, deep):
-        into = z_buffers(b)[1]
-        landed(into.at[b], z_recv.at[b])
-        value = value + into[b].astype(jnp.float32)
-    gq_ref[...] = value
+        gp_ref[:, ks] = (
+            jnp.dot(grad[:own, :], q_all[:, ks], preferred_element_type=jnp.float32) + gp_in[:, ks]
+        )
+
+    for k in mix:
+        settle(deep - 1, k)
+        value = plane[:, area(k)]
+        for n in range(deep - 1):
+            into = z_buffers(n)[1]
+            landed(into.at[targets[n], :, area(k)], z_recv.at[targets[n], k])
+            value = value + into[targets[n], :, area(k)].astype(jnp.float32)
+        gq_ref[:, area(k)] = value
+    for n in range(deep):
+        for side in range(2):
+            for sem in (rd_send, ru_send, rm_send):
+                waits.append((None, merge_x.at[n], sem.at[n, side]))
+        if n < deep - 1:
+            waits.append((None, z_buffers(n)[0].at[n], z_send.at[n]))
     for inside, ref, sem in waits:
         if inside is None:
             landed(ref, sem)
@@ -429,6 +479,17 @@
             pl.when(inside)(functools.partial(landed, ref, sem))
     for copy in sent:
         copy.wait_send()
+
+
+def store_kernel(loss_ref, gq_ref, gp_ref, loss_out, gq_out, gp_out, sems):
+    copies = [
+        pltpu.make_async_copy(source, out, sems.at[n])
+        for n, (source, out) in enumerate(((gp_ref, gp_out), (gq_ref, gq_out), (loss_ref, loss_out)))
+    ]
+    for copy in copies:
+        copy.start()
+    for copy in copies:
+        copy.wait()
 
 
 def on_device(queries, passages, positives, hard_negatives, thresholds):
@@ -439,7 +500,7 @@
     own = passages.shape[0]
     negs = hard_negatives.shape[1]
     run = deep * wide * block
-    fits = rows == 2 and columns % (cores * wide) == 0 and deep > 1
+    fits = rows == 2 and columns % (cores * wide) == 0 and deep > 1 and deep % 2 == 0
     fits = fits and block % 16 == 0 and run % lane == 0 and negs <= fields // 2 and depth % 1024 == 0
     if not fits:
         return general_plan(queries, passages, positives, hard_negatives, thresholds)
@@ -448,10 +509,10 @@
     half = depth // 2
     low, full = jnp.bfloat16, jnp.float32
     dma = pltpu.SemaphoreType.DMA
-    losses, grad_queries, grad_passages = pl.pallas_call(
+    results = pl.pallas_call(
         functools.partial(step_kernel, rows, wide, deep, negs),
         out_shape=(
-            jax.ShapeDtypeStruct((1, lane), full),
+            jax.ShapeDtypeStruct((1, block), full),
             jax.ShapeDtypeStruct((block, depth), full),
             jax.ShapeDtypeStruct((own, depth), full),
         ),
@@ -468,10 +529,10 @@
             pltpu.VMEM((fields, run), full),
             pltpu.VMEM((rows, fields, run), full),
             pltpu.VMEM((cores * own, total), full),
+            pltpu.VMEM((1, 2 * total), full),
+            pltpu.VMEM((groups, 1, 2 * total), full),
             pltpu.VMEM((1, total), full),
             pltpu.VMEM((groups, 1, total), full),
-            pltpu.VMEM((1, 2 * total), full),
-            pltpu.VMEM((groups, 1, 2 * total), full),
             pltpu.VMEM((total, depth), full),
             pltpu.VMEM((total, depth), low),
             pltpu.VMEM((own, depth), full),
@@ -490,14 +551,26 @@
             dma((5,)), dma((4,)), dma((2, deep, 3)), dma((2, deep, 2)), dma((groups, 4)),
             dma((2,)), dma((2,)), dma, dma,
             dma((groups,)), dma((groups,)), dma((groups,)), dma((groups,)),
-            dma((deep, 2)), dma((deep, 2)), dma((deep, 2)), dma((deep, 2)),
-            dma((deep, 2)), dma((deep, 2)), dma((deep,)), dma((deep,)),
+            dma((deep, 2)), dma((deep, 4)), dma((deep, 2)), dma((deep, 4)),
+            dma((deep, 2)), dma((deep, 4)), dma((deep,)), dma((deep, 4)),
+            pltpu.SemaphoreType.REGULAR,
         ],
         compiler_params=pltpu.CompilerParams(
             collective_id=0, has_side_effects=True, vmem_limit_bytes=44 * 1024 * 1024
         ),
-    )(queries, passages, positives[None], hard_negatives.T, thresholds[None])
-    return (losses[0, :block], grad_queries, grad_passages)
+    )(*(
+        pltpu.with_memory_space_constraint(a, pltpu.HBM)
+        for a in (queries, passages, positives[None], hard_negatives.T, thresholds[None])
+    ))
+    losses, grad_queries, grad_passages = pl.pallas_call(
+        store_kernel,
+        out_shape=[jax.ShapeDtypeStruct(a.shape, a.dtype) for a in results],
+        in_specs=[pl.BlockSpec(memory_space=pltpu.VMEM)] * 3,
+        out_specs=[pl.BlockSpec(memory_space=pltpu.HBM)] * 3,
+        scratch_shapes=[dma((3,))],
+        compiler_params=pltpu.CompilerParams(vmem_limit_bytes=8 * 1024 * 1024),
+    )(*results)
+    return (losses[0], grad_queries, grad_passages)
 
 
 def solution(mesh):

time: 69.9 us -> 59.1 us (0.85)
  local copies, waits for them, and re-layouts: 7.77 us -> 0 us
  Pallas kernels: 61.3 us -> 58.3 us
    unnamed x12 -> x0, local copies, waits for them, and re-layouts: 7.26 us -> none
    pallas_call x1, Pallas kernels: 61.3 us -> 56.2 us  [on_device(): pl.pallas_call(functools.partial(step_kernel, rows, wide, deep, negs), ou...]
    pallas_call x0 -> x1, Pallas kernels: none -> 2.11 us  [on_device(): pl.pallas_call(store_kernel, out_shape=[jax.ShapeDtypeStruct(a.shape, a.d...]
where the time goes in v2:
time: 59.1 us; the launch traced here: 58.9 us
  Pallas kernels  58.3 us (99%)
  between operations  0.64 us (1%)
    pallas_call x1, Pallas kernels, on_device(): pl.pallas_call(functools.partial(step_kernel, rows, wide, deep, negs), ou...  56.2 us
    pallas_call x1, Pallas kernels, on_device(): pl.pallas_call(store_kernel, out_shape=[jax.ShapeDtypeStruct(a.shape, a.d...  2.11 us

profile of v2, /device:TPU:0, one launch (start us, length us, event | category | flops | bytes accessed | tf_op | source)
XLA Modules:
  0.0 58.9 jit_solution(18080489222422890272)
XLA Ops:
  0.6 56.2 %shard_map.76 = (f32[1,16]{1,0:T(1,128)S(1)}, f32[16,4096]{1,0:T(8,128)S(1)}, f32[256,4096]{1,0:T(8,128)S(1)}) custom-call(bf16[16,4096]{1,0:T(8,128)(2,1)} %q_ref.1, bf16[256,4096]{1,0:T(8,128)(2,1)} %p_ref.1, s32[1,256]{1,0:T(1,128)} %bitcast.5, s32[7,256]{1,0:T(8,128)} %bitcast.4, f32[1,256]{1,0:T(1,128)} %bitcast.6), custom_call_target="tpu_custom_call" | custom-call | tf_op jit(solution)/shard_map/pallas_call | solution.py:512
  56.8 2.1 %shard_map.77 = (f32[1,16]{1,0:T(1,128)}, f32[16,4096]{1,0:T(8,128)}, f32[256,4096]{1,0:T(8,128)}) custom-call(f32[1,16]{1,0:T(1,128)S(1)} %get-tuple-element.9.loss_ref, f32[16,4096]{1,0:T(8,128)S(1)} %get-tuple-element.10.gq_ref, f32[256,4096]{1,0:T(8,128)S(1)} %get-tuple-element.11.gp_ref), custom_call_target="tpu_custom_call" | custom-call | tf_op jit(solution)/shard_map/pallas_call | solution.py:565

commit v3 on v2

--- a/solution.py
+++ b/solution.py
@@ -397,7 +397,7 @@
         )
 
     def z_buffers(n):
-        return (z_out_full, z_in_full) if n >= deep // 2 else (z_out, z_in)
+        return (z_out_full, z_in_full) if n >= deep else (z_out, z_in)
 
     def settle(n, k):
         landed((in_y if k < per else in_x).at[n, :, area(k)], ru_recv.at[n, k])

time: 59.1 us -> 57.7 us (0.976)
  Pallas kernels: 58.3 us -> 56.9 us
    pallas_call x1, Pallas kernels: 56.2 us -> 54.8 us  [on_device(): pl.pallas_call(functools.partial(step_kernel, rows, wide, deep, negs), ou...]
where the time goes in v3:
time: 57.7 us; the launch traced here: 57.5 us
  Pallas kernels  56.9 us (99%)
  between operations  0.64 us (1%)
    pallas_call x1, Pallas kernels, on_device(): pl.pallas_call(functools.partial(step_kernel, rows, wide, deep, negs), ou...  54.8 us
    pallas_call x1, Pallas kernels, on_device(): pl.pallas_call(store_kernel, out_shape=[jax.ShapeDtypeStruct(a.shape, a.d...  2.11 us

profile of v3, /device:TPU:0, one launch (start us, length us, event | category | flops | bytes accessed | tf_op | source)
XLA Modules:
  0.0 57.5 jit_solution(2829900509794951061)
XLA Ops:
  0.6 54.8 %shard_map.76 = (f32[1,16]{1,0:T(1,128)S(1)}, f32[16,4096]{1,0:T(8,128)S(1)}, f32[256,4096]{1,0:T(8,128)S(1)}) custom-call(bf16[16,4096]{1,0:T(8,128)(2,1)} %q_ref.1, bf16[256,4096]{1,0:T(8,128)(2,1)} %p_ref.1, s32[1,256]{1,0:T(1,128)} %bitcast.5, s32[7,256]{1,0:T(8,128)} %bitcast.4, f32[1,256]{1,0:T(1,128)} %bitcast.6), custom_call_target="tpu_custom_call" | custom-call | tf_op jit(solution)/shard_map/pallas_call | solution.py:512
  55.4 2.1 %shard_map.77 = (f32[1,16]{1,0:T(1,128)}, f32[16,4096]{1,0:T(8,128)}, f32[256,4096]{1,0:T(8,128)}) custom-call(f32[1,16]{1,0:T(1,128)S(1)} %get-tuple-element.9.loss_ref, f32[16,4096]{1,0:T(8,128)S(1)} %get-tuple-element.10.gq_ref, f32[256,4096]{1,0:T(8,128)S(1)} %get-tuple-element.11.gp_ref), custom_call_target="tpu_custom_call" | custom-call | tf_op jit(solution)/shard_map/pallas_call | solution.py:565

commit v4 on v3

--- a/solution.py
+++ b/solution.py
@@ -73,7 +73,7 @@
     rows, wide, deep, negs,
     q_ref, p_ref, positives_ref, mined_ref, thresholds_ref,
     loss_ref, gq_ref, gp_ref,
-    p_own, positives_own, mined_own, thresholds_own,
+    positive_mask, kept_mask, margin, grown_t, positive_t, p_own, positives_own, mined_own, thresholds_own,
     q_all, p_mate, mined_wide, meta_ref, meta_all, scores, pick_out, pick_all, stat_out, stat_all,
     part, part_low, gp_out, gp_in,
     diag_in_y, diag_in_x, merge_x, merge_y, in_x, in_y, plane, z_out, z_in, z_out_full, z_in_full,
@@ -124,9 +124,22 @@
     me = slot(y, z, x)
     mate = device(y, z, x, 1 - core)
     across, along = device(y, z, xn), device(yn, z, x)
+    low_half = z < deep // 2
+    folded = jnp.where(low_half, z, deep - 1 - z)
+
+    def target(n):
+        if n == deep - 1:
+            return z
+        v = deep - 1 - n
+        v = jnp.where(v > folded, v, v - 1)
+        return jnp.where(low_half, v, deep - 1 - v)
+
+    targets = [target(n) for n in range(deep)]
+
     peers = [
-        (turn(y, a, rows), turn(z, b, deep), turn(x, d, wide))
-        for b in range(deep) for a in range(rows) for d in range(wide) if a + b + d
+        (yy, zz, xx)
+        for n, zz in enumerate(targets)
+        for yy, xx in ((yn, xn), (yn, x), (y, xn), (y, x))[: 4 if n < deep - 1 else 3]
     ]
     steps = 4
     width = depth // steps
@@ -257,6 +270,21 @@
         waits.append((inside, q_all.at[span(me), left], sem.at[0]))
         waits.append((inside, q_all.at[span(me), left], sem.at[1]))
         return forward
+
+    def masks():
+        landed(meta_all.at[yn], meta_recv)
+        mt = jnp.concatenate([meta_all[a] for a in range(rows)], axis=1)
+        at = lax.broadcasted_iota(jnp.int32, (2 * own, queries), 0)
+        first = ((chip * cores + core) * rows + y) * own
+        second = ((chip * cores + (1 - core)) * rows + y) * own
+        ids = jnp.where(at < own, at + first, at - own + second).astype(jnp.float32)
+        positive = ids == mt[fields // 2 : fields // 2 + 1, :]
+        kept = positive
+        for n in range(negs):
+            kept = kept | (ids == mt[n : n + 1, :])
+        positive_mask[...] = positive.astype(jnp.float32)
+        kept_mask[...] = kept.astype(jnp.float32)
+        margin[...] = mt[fields // 2 + 1 : fields // 2 + 2, :]
 
     corners = [corner_step(z, None, diag_send.at[0, 0])]
     for h in range(1, deep):
@@ -271,6 +299,8 @@
             def _():
                 pl.semaphore_signal(turn_sem, inc=1, device_id=mate, device_id_type=MESH)
 
+        if h == 1:
+            masks()
         corners = [
             corner_step(z - h, z - h >= 0, diag_send.at[0, h]),
             corner_step(z + h, z + h < deep, diag_send.at[1, h]),
@@ -279,7 +309,6 @@
         for go in corners:
             go(k)
     landed(p_mate, mate_recv.at[0])
-    landed(meta_all.at[yn], meta_recv)
 
     for k in range(steps):
         for b in range(deep):
@@ -299,17 +328,10 @@
             else:
                 scores[at : at + own, :] = value
 
-    mt = jnp.concatenate([meta_all[a] for a in range(rows)], axis=1)
-    at = lax.broadcasted_iota(jnp.int32, (2 * own, queries), 0)
-    first = ((chip * cores + core) * rows + y) * own
-    second = ((chip * cores + (1 - core)) * rows + y) * own
-    ids = jnp.where(at < own, at + first, at - own + second).astype(jnp.float32)
     sc = scores[...] * inv_temp
-    positive = ids == mt[fields // 2 : fields // 2 + 1, :]
+    positive = positive_mask[...] > 0.0
     picked_here = jnp.sum(jnp.where(positive, sc, 0.0), axis=0, keepdims=True)
-    kept = positive
-    for n in range(negs):
-        kept = kept | (ids == mt[n : n + 1, :])
+    kept = kept_mask[...] > 0.0
     held_here = jnp.max(jnp.where(kept, sc, -jnp.inf), axis=0, keepdims=True)
     pick_out[...] = jnp.concatenate([picked_here, held_here], axis=1)
     for n, peer in enumerate(peers):
@@ -321,7 +343,7 @@
     picks = pick_all[...]
     picked = jnp.sum(picks[:, :, :queries], axis=0)
     held = jnp.max(picks[:, :, queries:], axis=0)
-    v = sharpness * (sc - picked - mt[fields // 2 + 1 : fields // 2 + 2, :])
+    v = sharpness * (sc - picked - margin[...])
     penalty = jnp.maximum(v, 0.0) + jnp.log1p(jnp.exp(-jnp.abs(v)))
     grown = jnp.exp(jnp.where(kept, sc, sc - penalty) - held)
     sum_here = jnp.sum(grown, axis=0, keepdims=True)
@@ -329,15 +351,15 @@
     for n, peer in enumerate(peers):
         send(stat_out, stat_all.at[me], stat_send.at[n], stat_recv.at[me], device(*peer))
     stat_all[me] = sum_here
+    grown_t[...] = jnp.transpose(grown)
+    positive_t[...] = jnp.transpose(positive_mask[...])
     for peer in peers:
         g = slot(*peer)
         landed(stat_all.at[g], stat_recv.at[g])
     total = jnp.sum(stat_all[...], axis=0)
-    losses = jnp.broadcast_to(held + jnp.log(total) - picked, (8, queries))
-    loss_ref[...] = pltpu.roll(losses, lax.rem(queries - me * block, queries), 1)[:1, :block]
     factor = 1.0 / total
-    grad = ((grown * factor - positive.astype(jnp.float32)) * inv_temp).astype(jnp.bfloat16)
-    grad_t = jnp.transpose(grad)
+    factor_t = jnp.transpose(jnp.broadcast_to(factor, (8, queries)))[:, :1]
+    grad_t = ((grown_t[...] * factor_t - positive_t[...]) * inv_temp).astype(jnp.bfloat16)
 
     cuts = 8
     cut = depth // cuts
@@ -345,18 +367,6 @@
     share = depth // parts
     per = parts // 2
     mix = [k for pair in zip(range(per), range(per, parts)) for k in pair]
-    low_half = z < deep // 2
-    folded = jnp.where(low_half, z, deep - 1 - z)
-
-    def target(n):
-        if n == deep - 1:
-            return z
-        v = deep - 1 - n
-        v = jnp.where(v > folded, v, v - 1)
-        return jnp.where(low_half, v, deep - 1 - v)
-
-    targets = [target(n) for n in range(deep)]
-
     def area(k, wrap=False):
         return pl.ds((k % per if wrap else k) * share, share)
 
@@ -429,6 +439,10 @@
         diagonal(1, k)
     for k in mix:
         plain(0, k)
+
+    losses = jnp.broadcast_to(held + jnp.log(total) - picked, (8, queries))
+    loss_ref[...] = pltpu.roll(losses, lax.rem(queries - me * block, queries), 1)[:1, :block]
+    grad = ((grown * factor - positive.astype(jnp.float32)) * inv_temp).astype(jnp.bfloat16)
 
     @pl.loop(0, cuts)
     def _(k):
@@ -519,6 +533,11 @@
         in_specs=[pl.BlockSpec(memory_space=pltpu.HBM)] * 5,
         out_specs=[pl.BlockSpec(memory_space=pltpu.VMEM)] * 3,
         scratch_shapes=[
+            pltpu.VMEM((cores * own, total), full),
+            pltpu.VMEM((cores * own, total), full),
+            pltpu.VMEM((1, total), full),
+            pltpu.VMEM((total, cores * own), full),
+            pltpu.VMEM((total, cores * own), full),
             pltpu.VMEM((own, depth), low),
             pltpu.VMEM((1, positives.shape[0]), jnp.int32),
             pltpu.VMEM((negs, positives.shape[0]), jnp.int32),
@@ -556,7 +575,7 @@
             pltpu.SemaphoreType.REGULAR,
         ],
         compiler_params=pltpu.CompilerParams(
-            collective_id=0, has_side_effects=True, vmem_limit_bytes=44 * 1024 * 1024
+            collective_id=0, has_side_effects=True, vmem_limit_bytes=46 * 1024 * 1024
         ),
     )(*(
         pltpu.with_memory_space_constraint(a, pltpu.HBM)

time: 57.7 us -> 57.5 us (level)
  no operation moved by 1% of the time
where the time goes in v4:
time: 57.5 us; the launch traced here: 57.3 us
  Pallas kernels  56.7 us (99%)
  between operations  0.64 us (1%)
    pallas_call x1, Pallas kernels, on_device(): pl.pallas_call(functools.partial(step_kernel, rows, wide, deep, negs), ou...  54.6 us
    pallas_call x1, Pallas kernels, on_device(): pl.pallas_call(store_kernel, out_shape=[jax.ShapeDtypeStruct(a.shape, a.d...  2.11 us

profile of v4, /device:TPU:0, one launch (start us, length us, event | category | flops | bytes accessed | tf_op | source)
XLA Modules:
  0.0 57.3 jit_solution(10472870401076590824)
XLA Ops:
  0.6 54.6 %shard_map.76 = (f32[1,16]{1,0:T(1,128)S(1)}, f32[16,4096]{1,0:T(8,128)S(1)}, f32[256,4096]{1,0:T(8,128)S(1)}) custom-call(bf16[16,4096]{1,0:T(8,128)(2,1)} %q_ref.1, bf16[256,4096]{1,0:T(8,128)(2,1)} %p_ref.1, s32[1,256]{1,0:T(1,128)} %bitcast.5, s32[7,256]{1,0:T(8,128)} %bitcast.4, f32[1,256]{1,0:T(1,128)} %bitcast.6), custom_call_target="tpu_custom_call" | custom-call | tf_op jit(solution)/shard_map/pallas_call | solution.py:526
  55.2 2.1 %shard_map.77 = (f32[1,16]{1,0:T(1,128)}, f32[16,4096]{1,0:T(8,128)}, f32[256,4096]{1,0:T(8,128)}) custom-call(f32[1,16]{1,0:T(1,128)S(1)} %get-tuple-element.9.loss_ref, f32[16,4096]{1,0:T(8,128)S(1)} %get-tuple-element.10.gq_ref, f32[256,4096]{1,0:T(8,128)S(1)} %get-tuple-element.11.gp_ref), custom_call_target="tpu_custom_call" | custom-call | tf_op jit(solution)/shard_map/pallas_call | solution.py:584
